TPU v7x, 32 devices: a whole 2x2x4 slice. The times are simulated.
32 devices in a mesh: replica: 8 (over z, core), ctx: 4 (over y, x).
Axes of the slice: x: 2, y: 2, z: 4, core: 2. Of those that a mesh axis runs over, the one named last changes fastest.
Arguments:
- queries: bfloat16 [32, 128, 3584], P('replica', 'ctx'), may hold values from -128 to 128
- key_cache: bfloat16 [4096, 512], P('ctx'), may hold values from -6 to 6
- value_cache: bfloat16 [4096, 512], P('ctx'), may hold values from -6 to 6
- key_scale: float32 [32, 4], P('ctx'), may hold values from 0.7 to 1.4
- value_scale: float32 [32, 4], P('ctx'), may hold values from 0.5 to 2
- pattern: int32 [28, 32, 32], replicated, may hold values from 0 to 31
- target: int32 [32], replicated, may hold values from 0 to 7, as said below
Outputs:
- landed: bfloat16 [32, 128, 3584], P('replica', 'ctx')
Inputs may be any that keep to these rules, and one draw needn't show every extreme that they name: `target`: query block j belongs to group j // 4. The blocks of one group go to distinct groups, and every group receives exactly 4 blocks.
All inputs are finite; a program needn't handle non-finite values.
Results may differ from a plain program's by a relative error of at most 0.018.
Values may be sent and summed in bfloat16 or wider, within the bound.
No kernel may reach another device: no remote copies, remote signals or barrier semaphores. Data moves between devices by JAX's collectives and lax.ppermute only.
A program may use at most 64 MiB of HBM per device.

v0:
```python
import math
import jax
import jax.numpy as jnp
from jax import lax
from jax.sharding import PartitionSpec as P


def arrivals(target, group_index, group_count, per_group):
    block_grid = target.reshape(group_count, per_group)
    hit_table = (block_grid == group_index).astype(jnp.int32)
    coming = jnp.sum(hit_table, axis=1)
    arrival_slot = jnp.cumsum(coming) - 1
    places = jnp.arange(per_group, dtype=jnp.int32)
    matched = (coming[None, :] > 0) & (arrival_slot[None, :] == places[:, None])
    anchor = jnp.arange(group_count, dtype=jnp.int32) * per_group + jnp.sum(
        hit_table * places[None, :], axis=1
    )
    arriving = jnp.sum(jnp.where(matched, anchor[None, :], 0), axis=1)
    return (matched.astype(jnp.bfloat16), arriving)


def relocate(blocks, target, group_index, group_count, per_group, picker):
    own_targets = lax.dynamic_slice_in_dim(target, group_index * per_group, per_group)
    outgoing = (own_targets[None, :] == jnp.arange(group_count, dtype=jnp.int32)[:, None]).astype(
        jnp.bfloat16
    )
    packed = jnp.einsum("dk,kxh->dxh", outgoing, blocks, preferred_element_type=jnp.float32).astype(
        jnp.bfloat16
    )
    received = lax.all_to_all(packed, "replica", split_axis=0, concat_axis=0, tiled=True)
    return jnp.einsum("sr,rxh->sxh", picker, received, preferred_element_type=jnp.float32).astype(
        jnp.bfloat16
    )


def collect(blocks):
    return lax.all_gather(blocks, "ctx", axis=1, tiled=True)


def attend(
    whole,
    block_list,
    key_cache,
    value_cache,
    key_scale,
    value_scale,
    pattern,
    shard_index,
    kv_blocks,
):
    block_count, block_rows, row_width = whole.shape
    kv_heads = key_scale.shape[1]
    head_size = key_cache.shape[1] // kv_heads
    head_count = row_width // head_size
    group_size = head_count // kv_heads
    local_blocks = key_cache.shape[0] // block_rows
    first_block = kv_blocks - pattern.shape[1]
    query = whole.reshape(block_count, block_rows, kv_heads, group_size, head_size)
    keys = key_cache.reshape(local_blocks, block_rows, kv_heads, head_size)
    values = value_cache.reshape(local_blocks, block_rows, kv_heads, head_size)
    listed = jnp.take(pattern, block_list, axis=1).reshape(
        kv_heads, group_size, block_count, pattern.shape[2]
    )
    diagonal = first_block + block_list
    row_ids = jnp.arange(block_rows, dtype=jnp.int32)
    block_ids = shard_index * local_blocks + jnp.arange(local_blocks, dtype=jnp.int32)
    key_pos = block_ids[:, None] * block_rows + row_ids[None, :]
    inv_root = 1.0 / math.sqrt(head_size)

    def one_item(item):
        block_slot = item // kv_heads
        head = item % kv_heads
        query_tile = lax.dynamic_index_in_dim(
            lax.dynamic_index_in_dim(query, block_slot, 0, keepdims=False), head, 1, keepdims=False
        )
        key_head = lax.dynamic_index_in_dim(keys, head, 2, keepdims=False)
        value_head = lax.dynamic_index_in_dim(values, head, 2, keepdims=False)
        heads_listed = lax.dynamic_index_in_dim(
            lax.dynamic_index_in_dim(listed, head, 0, keepdims=False), block_slot, 1, keepdims=False
        )
        diag = lax.dynamic_index_in_dim(diagonal, block_slot, 0, keepdims=False)
        chosen = (
            jnp.any(heads_listed[:, :, None] == block_ids[None, None, :], axis=1)
            | (block_ids == diag)[None, :]
        )
        query_pos = diag * block_rows + row_ids
        causal = key_pos[None, :, :] <= query_pos[:, None, None]
        allowed = chosen[:, None, :, None] & causal[None]
        key_factor = lax.dynamic_index_in_dim(key_scale, head, 1, keepdims=False) * inv_root
        value_factor = lax.dynamic_index_in_dim(value_scale, head, 1, keepdims=False)
        product = jnp.einsum(
            "rkd,btd->krbt", query_tile, key_head, preferred_element_type=jnp.float32
        )
        scores = product * key_factor[None, None, :, None]
        local_top = jnp.max(jnp.where(allowed, scores, -jnp.inf), axis=(2, 3))
        expo = jnp.where(allowed, jnp.exp(scores - local_top[:, :, None, None]), 0.0)
        weight = (expo * value_factor[None, None, :, None]).astype(jnp.bfloat16)
        numer = jnp.einsum("krbt,btd->rkd", weight, value_head, preferred_element_type=jnp.float32)
        denom = jnp.transpose(jnp.sum(expo, axis=(2, 3)))
        return (numer, denom, jnp.transpose(local_top))

    numer_all, denom_all, top_all = lax.map(
        one_item, jnp.arange(block_count * kv_heads, dtype=jnp.int32)
    )
    numer_all = numer_all.reshape(block_count, kv_heads, block_rows, group_size, head_size)
    denom_all = denom_all.reshape(block_count, kv_heads, block_rows, group_size)
    local_top = top_all.reshape(block_count, kv_heads, block_rows, group_size)
    top_score = lax.pmax(local_top.astype(jnp.bfloat16), "ctx").astype(local_top.dtype)
    rescale = jnp.exp(local_top - top_score)
    numer_scaled = jnp.transpose(numer_all * rescale[..., None], (0, 2, 1, 3, 4)).reshape(
        block_count, block_rows, row_width
    )
    denom_scaled = jnp.transpose(denom_all * rescale, (0, 2, 1, 3)).reshape(
        block_count, block_rows, head_count
    )
    numer_sum, denom_sum = (
        lax.psum_scatter(
            numer_scaled.astype(jnp.bfloat16), "ctx", scatter_dimension=1, tiled=True
        ).astype(jnp.float32),
        lax.psum_scatter(
            denom_scaled.astype(jnp.bfloat16), "ctx", scatter_dimension=1, tiled=True
        ).astype(jnp.float32),
    )
    own_rows = numer_sum.shape[1]
    attended = (
        numer_sum.reshape(block_count, own_rows, head_count, head_size) / denom_sum[..., None]
    )
    return attended.reshape(block_count, own_rows, row_width).astype(jnp.bfloat16)


def per_device(queries, key_cache, value_cache, key_scale, value_scale, pattern, target):
    group_count = lax.axis_size("replica")
    shard_count = lax.axis_size("ctx")
    group_index = lax.axis_index("replica")
    shard_index = lax.axis_index("ctx")
    per_group = queries.shape[0]
    block_rows = queries.shape[1] * shard_count
    kv_blocks = key_cache.shape[0] // block_rows * shard_count
    picker, arriving = arrivals(target, group_index, group_count, per_group)
    moved = relocate(queries, target, group_index, group_count, per_group, picker)
    whole = collect(moved)
    return attend(
        whole,
        arriving,
        key_cache,
        value_cache,
        key_scale,
        value_scale,
        pattern,
        shard_index,
        kv_blocks,
    )


def solution(mesh):
    return jax.shard_map(
        per_device,
        mesh=mesh,
        in_specs=(
            P("replica", "ctx", None),
            P("ctx", None),
            P("ctx", None),
            P("ctx", None),
            P("ctx", None),
            P(),
            P(),
        ),
        out_specs=P("replica", "ctx", None),
        check_vma=False,
    )
```

profile of v0, /device:TPU:0, one launch (start us, length us, event | category | flops | bytes accessed | tf_op | source)
XLA Modules:
  0.0 480.7 jit_solution(8024060534990406194)
XLA Ops:
  10.5 6.4 %all-to-all-start = ((bf16[8,32,3584]{2,1,0:T(8,128)(2,1)}), bf16[8,32,3584]{2,1,0:T(8,128)(2,1)S(1)}, u32[]{:S(2)}, u32[]{:S(2)}) async-start(bf16[8,32,3584]{2,1,0:T(8,128)(2,1)} %copy.52), calls=%async_computation | async-start | bytes 3670016 | tf_op jit(solution)/shard_map/all_to_all | solution.py:30
  17.4 42.9 %all-to-all-done = bf16[8,32,3584]{2,1,0:T(8,128)(2,1)S(1)} async-done(((bf16[8,32,3584]{2,1,0:T(8,128)(2,1)}), bf16[8,32,3584]{2,1,0:T(8,128)(2,1)S(1)}, u32[]{:S(2)}, u32[]{:S(2)}) %all-to-all-start) | async-done | bytes 1835040 | tf_op jit(solution)/shard_map/all_to_all | solution.py:30
  67.8 42.8 %all-gather.2.cloned.1.call-done = bf16[4,128,3584]{2,0,1:T(4,128)(2,1)} async-done(((bf16[4,32,3584]{2,0,1:T(4,128)(2,1)}), bf16[4,128,3584]{2,0,1:T(4,128)(2,1)}) %all-gather.2.cloned.1.call-update) | async-done | bytes 3670032 | tf_op jit(solution)/shard_map/all_gather | solution.py:37
  110.6 7.2 %copy.54 = bf16[4,128,3584]{1,2,0:T(8,128)(2,1)} copy(bf16[4,128,3584]{2,0,1:T(4,128)(2,1)} %all-gather.2.cloned.1.call-done) | data formatting | bytes 7340032 | tf_op jit(solution)/shard_map/all_gather | solution.py:37
  117.8 209.7 %while.18 = (s32[]{:T(128)}, f32[16,128,7,128]{1,3,2,0:T(8,128)}, f32[16,128,7]{1,2,0:T(8,128)S(1)}, f32[16,128,7]{1,2,0:T(8,128)S(1)}, s32[16]{0:T(128)S(1)}, /...) while((s32[]{:T(128)}, f32[16,128,7,128]{1,3,2,0:T(8,128)}, ...), condition=%wide.region_8.9_spmd.clone, body=%wide.region_4.8_spmd.clone.sunk | while | flops 483658688 | bytes 12792716 | solution.py:102
  127.8 3.1 fusion.47
  140.9 3.1 fusion.47
  154.1 3.1 fusion.47
  167.2 3.1 fusion.47
  180.3 3.1 fusion.47
  193.4 3.1 fusion.47
  206.5 3.1 fusion.47
  219.6 3.0 fusion.47
  232.7 3.1 fusion.47
  245.8 3.1 fusion.47
  272.0 3.1 fusion.47
  285.1 3.1 fusion.47
  311.3 3.1 fusion.47
  324.4 3.1 fusion.47
  327.5 15.4 %pmax.7 = bf16[4,4,128,7]{2,0,3,1:T(4,128)(2,1)S(1)} all-reduce(bf16[4,4,128,7]{2,0,3,1:T(4,128)(2,1)S(1)} %copy.87), channel_id=1, replica_groups=mesh['replica'=8,'ctx'=4] {'ctx'}, use_global_device_ids=true, to_apply=%region_9.10 | all-reduce | flops 14336 | bytes 57344 | tf_op jit(solution)/shard_map/pmax | solution.py:108
  347.0 6.2 %multiply_convert_fusion.6 = bf16[4,4,128,7,128]{2,4,3,1,0:T(8,128)(2,1)} fusion(f32[4,4,128,7,128]{2,4,3,1,0:T(8,128)} %bitcast.9, f32[4,4,128,7]{2,3,1,0:T(8,128)S(1)} %copy.60), kind=kLoop, calls=%fused_computation.39 | loop fusion | flops 3670016 | bytes 11067392 | tf_op jit(solution)/shard_map/convert_element_type | solution.py:118
  353.3 7.3 %copy.61 = bf16[4,128,3584]{2,0,1:T(4,128)(2,1)} copy(bf16[4,128,3584]{1,2,0:T(8,128)(2,1)} %bitcast.121) | data formatting | bytes 7340032 | tf_op jit(solution)/shard_map/convert_element_type | solution.py:118
  362.6 8.6 %reduce-scatter.4.cloned.1.call-done = bf16[32,112]{1,0:T(8,128)(2,1)} async-done(((bf16[128,112]{1,0:T(8,128)(2,1)}), bf16[32,112]{1,0:T(8,128)(2,1)}) %reduce-scatter.4.cloned.1.call-update) | async-done | bytes 7184
  375.1 94.9 %all-reduce.3.cloned.1.call-done = bf16[4,128,3584]{2,0,1:T(4,128)(2,1)} async-done(((bf16[4,128,3584]{2,0,1:T(4,128)(2,1)}), bf16[4,128,3584]{2,0,1:T(4,128)(2,1)}) %all-reduce.3.cloned.1.call-update) | async-done | bytes 3670032
  (315 shorter events, 138.4 us)
Async XLA Ops:
  6.5 1.2 copy-start
  8.7 8.2 %copy-start.4 = (s32[32]{0:T(128)S(1)}, s32[32]{0:T(128)}, u32[]{:S(2)}) copy-start(s32[32]{0:T(128)} %param.15) | copy-start | bytes 388
  10.5 49.8 %all-to-all-start = ((bf16[8,32,3584]{2,1,0:T(8,128)(2,1)}), bf16[8,32,3584]{2,1,0:T(8,128)(2,1)S(1)}, u32[]{:S(2)}, u32[]{:S(2)}) async-start(bf16[8,32,3584]{2,1,0:T(8,128)(2,1)} %copy.52), calls=%async_computation | async-start | bytes 3670016 | tf_op jit(solution)/shard_map/all_to_all | solution.py:30
  16.9 93.7 %all-gather.2.cloned.1.call-start = ((), (), s32[]{:S(2)}) async-start(), calls=%async_computation.2 | async-start | bytes 4587520 | tf_op jit(solution)/shard_map/all_gather | solution.py:37
  63.2 3.0 copy-start.1
  63.3 307.9 %reduce-scatter.4.cloned.1.call-start = ((), (), s32[]{:S(2)}) async-start(), calls=%async_computation.3 | async-start | bytes 40960
  64.8 2.1 copy-start.2
  67.7 50.1 %copy-start.3 = (f32[16,128,7]{1,2,0:T(8,128)S(1)}, f32[16,128,7]{1,2,0:T(8,128)}, u32[]{:S(2)}) copy-start(f32[16,128,7]{1,2,0:T(8,128)} %custom-call.3) | copy-start | bytes 172036
  347.0 123.0 %all-reduce.3.cloned.1.call-start = ((), (), s32[]{:S(2)}) async-start(), calls=%async_computation.4 | async-start | bytes 7340032
  360.6 0.7 copy-start.5
Sparse Core Ops, SparseCore 0:
  63.4 47.1 all-gather.1
  347.1 23.9 reduce-scatter.3
  374.2 95.6 all-reduce.2
where the time goes:
time: 484 us; the launch traced here: 481 us
  waiting for transfers between devices  189 us (39%)
  matrix products  80.3 us (17%)
  local copies, waits for them, and re-layouts  63.9 us (13%)
  other arithmetic  57.7 us (12%)
  loops' own time  53.7 us (11%)
  blocking collectives  15.4 us (3%)
  between operations  14 us (3%)
  starting transfers between devices  6.47 us (1%)
    unnamed x5, waiting for transfers between devices  104 us
    another operation x1, loops' own time, attend(): lax.map(one_item, jnp.arange(block_count * kv_heads, dtype=jnp.int32))  53.7 us
    dot_general x16, matrix products, one_item(): jnp.einsum('krbt,btd->rkd', weight, value_head, preferred_element_type=jn...  49 us
    all_to_all x1, waiting for transfers between devices, relocate(): lax.all_to_all(packed, 'replica', split_axis=0, concat_axis=0, tiled=True)  42.9 us
    all_gather x1, waiting for transfers between devices, collect(): return lax.all_gather(blocks, 'ctx', axis=1, tiled=True)  42.8 us
    dot_general x16, matrix products, one_item(): jnp.einsum('rkd,btd->krbt', query_tile, key_head, preferred_element_type=...  27.4 us
    reduce_sum x16, other arithmetic, one_item(): denom = jnp.transpose(jnp.sum(expo, axis=(2, 3)))  17.3 us
    pmax x1, blocking collectives, attend(): lax.pmax(local_top.astype(jnp.bfloat16), 'ctx').astype(local_top.dtype)  15.4 us
  transfers between devices with their start and end apart: 4, of which 4 were waited for; matrix products, arithmetic and copies ran while one was open for 5% of the time, Pallas kernels for 0%

commit v1 on v0

--- a/solution.py
+++ b/solution.py
@@ -3,6 +3,28 @@
 import jax.numpy as jnp
 from jax import lax
 from jax.sharding import PartitionSpec as P
+
+
+def classes_apply(buf, on_dim):
+    tmp = list(buf.shape[1:])
+    tmp[on_dim] *= buf.shape[0]
+    return jnp.moveaxis(buf, 0, on_dim).reshape(tmp)
+
+
+def bind_the_marks(field, which_axis):
+    tile_out = field[None]
+    n = lax.axis_size(which_axis)
+    for dd in range(n.bit_length() - 1):
+        shaped = 1 << dd
+        r_now = lax.ppermute(
+            tile_out,
+            axis_name=which_axis,
+            perm=list(map(lambda num: (num, num ^ shaped), range(n))),
+        )
+        m_next = jnp.stack([tile_out, r_now])
+        work_now = lax.axis_index(which_axis) >> dd & 1
+        tile_out = jnp.where(work_now == 0, m_next, m_next[::-1]).reshape(-1, *field.shape)
+    return tile_out
 
 
 def arrivals(target, group_index, group_count, per_group):
@@ -34,7 +56,11 @@
 
 
 def collect(blocks):
-    return lax.all_gather(blocks, "ctx", axis=1, tiled=True)
+
+    def search_routes_all_in(chunk, my_data, array_dim):
+        return classes_apply(bind_the_marks(chunk, my_data), array_dim)
+
+    return search_routes_all_in(blocks, "ctx", 1)
 
 
 def attend(

time: 484 us -> 525 us (1.085)
  local copies, waits for them, and re-layouts: 63.9 us -> 81.5 us
  other arithmetic: 57.7 us -> 67.6 us
    ppermute x0 -> x2, waiting for transfers between devices: none -> 49.5 us  [bind_the_marks(): lax.ppermute(tile_out, axis_name=which_axis, perm=list(map(lambda num: (n...]
    all_gather x1 -> x0, waiting for transfers between devices: 42.8 us -> none  [collect(): return lax.all_gather(blocks, 'ctx', axis=1, tiled=True)]
    unnamed x20 -> x19, local copies, waits for them, and re-layouts: 10.3 us -> 19.2 us
    another operation x0 -> x1, local copies, waits for them, and re-layouts: none -> 8.28 us  [attend(): whole.reshape(block_count, block_rows, kv_heads, group_size, head_size)]
    another operation x3 -> x6, other arithmetic: 0.19 us -> 8 us  [the longest x3 7.82 us: bind_the_marks(): m_next = jnp.stack([tile_out, r_now])]
    all_gather x1 -> x0, local copies, waits for them, and re-layouts: 7.22 us -> none  [collect(): return lax.all_gather(blocks, 'ctx', axis=1, tiled=True)]
    unnamed x5 -> x4, waiting for transfers between devices: 104 us -> 102 us
  transfers between devices with their start and end apart: 4 -> 5, of which waited for: 4 -> 5; matrix products, arithmetic and copies ran while one was open for 5% -> 6% of each run, Pallas kernels for 0% -> 0%
where the time goes in v1:
time: 525 us; the launch traced here: 521 us
  waiting for transfers between devices  194 us (37%)
  local copies, waits for them, and re-layouts  81.5 us (16%)
  matrix products  80.9 us (15%)
  other arithmetic  67.6 us (13%)
  loops' own time  57 us (11%)
  blocking collectives  16.3 us (3%)
  between operations  14.3 us (3%)
  starting transfers between devices  9.51 us (2%)
    unnamed x4, waiting for transfers between devices  102 us
    another operation x1, loops' own time, attend(): lax.map(one_item, jnp.arange(block_count * kv_heads, dtype=jnp.int32))  57 us
    ppermute x2, waiting for transfers between devices, bind_the_marks(): lax.ppermute(tile_out, axis_name=which_axis, perm=list(map(lambda num: (n...  49.5 us
    dot_general x16, matrix products, one_item(): jnp.einsum('krbt,btd->rkd', weight, value_head, preferred_element_type=jn...  49 us
    all_to_all x1, waiting for transfers between devices, relocate(): lax.all_to_all(packed, 'replica', split_axis=0, concat_axis=0, tiled=True)  42.9 us
    dot_general x16, matrix products, one_item(): jnp.einsum('rkd,btd->krbt', query_tile, key_head, preferred_element_type=...  28.9 us
    unnamed x19, local copies, waits for them, and re-layouts  19.2 us
    reduce_sum x16, other arithmetic, one_item(): denom = jnp.transpose(jnp.sum(expo, axis=(2, 3)))  17.3 us
  transfers between devices with their start and end apart: 5, of which 5 were waited for; matrix products, arithmetic and copies ran while one was open for 6% of the time, Pallas kernels for 0%

profile of v1, /device:TPU:0, one launch (start us, length us, event | category | flops | bytes accessed | tf_op | source)
XLA Modules:
  0.0 521.1 jit_solution(16512479463608945019)
XLA Ops:
  10.5 6.4 %all-to-all-start = ((bf16[8,32,3584]{2,1,0:T(8,128)(2,1)}), bf16[8,32,3584]{2,1,0:T(8,128)(2,1)S(1)}, u32[]{:S(2)}, u32[]{:S(2)}) async-start(bf16[8,32,3584]{2,1,0:T(8,128)(2,1)} %copy.51), calls=%async_computation | async-start | bytes 3670016 | tf_op jit(solution)/shard_map/all_to_all | solution.py:52
  17.4 42.9 %all-to-all-done = bf16[8,32,3584]{2,1,0:T(8,128)(2,1)S(1)} async-done(((bf16[8,32,3584]{2,1,0:T(8,128)(2,1)}), bf16[8,32,3584]{2,1,0:T(8,128)(2,1)S(1)}, u32[]{:S(2)}, u32[]{:S(2)}) %all-to-all-start) | async-done | bytes 1835040 | tf_op jit(solution)/shard_map/all_to_all | solution.py:52
  63.9 20.3 %collective-permute-done = bf16[1,4,32,3584]{3,1,2,0:T(4,128)(2,1)S(1)} collective-permute-done((bf16[1,4,32,3584]{3,1,2,0:T(4,128)(2,1)S(1)}, bf16[1,4,32,3584]{3,1,2,0:T(4,128)(2,1)S(1)}, u32[]{:S(2)}, u32[]{:S(2)}) %collective-permute-start) | collective-permute-done | bytes 917536 | tf_op jit(solution)/shard_map/ppermute | solution.py:19
  99.5 29.2 %collective-permute-done.1 = bf16[2,4,32,3584]{3,1,2,0:T(4,128)(2,1)} collective-permute-done((bf16[2,4,32,3584]{3,1,2,0:T(4,128)(2,1)}, bf16[2,4,32,3584]{3,1,2,0:T(4,128)(2,1)}, u32[]{:S(2)}, u32[]{:S(2)}) %collective-permute-start.1) | collective-permute-done | bytes 1835040 | tf_op jit(solution)/shard_map/ppermute | solution.py:19
  128.7 4.2 pad_maximum_fusion
  136.9 8.3 %reshape_reshape.3 = bf16[4,128,4,7,128]{4,3,2,1,0:T(8,128)(2,1)} reshape(bf16[4,4,32,3584]{3,2,1,0:T(8,128)(2,1)} %bitcast.134) | data formatting | bytes 7340032 | tf_op jit(solution)/shard_map/reshape;reshape | solution.py:84
  145.2 5.6 %copy.56 = bf16[4,128,4,7,128]{4,1,3,2,0:T(8,128)(2,1)} copy(bf16[4,128,4,7,128]{4,3,2,1,0:T(8,128)(2,1)} %reshape_reshape.3) | data formatting | bytes 7340032
  150.8 217.7 %while.18 = (s32[]{:T(128)}, f32[16,128,7,128]{1,3,2,0:T(8,128)}, f32[16,128,7]{1,2,0:T(8,128)S(1)}, f32[16,128,7]{1,2,0:T(8,128)S(1)}, s32[16]{0:T(128)S(1)}, /...) while((s32[]{:T(128)}, f32[16,128,7,128]{1,3,2,0:T(8,128)}, ...), condition=%wide.region_8.9_spmd.clone, body=%wide.region_4.8_spmd.clone.sunk | while | flops 483658688 | bytes 12791268 | solution.py:128
  175.0 3.1 fusion.49
  188.6 3.1 fusion.49
  202.2 3.1 fusion.49
  215.8 3.1 fusion.49
  243.0 3.1 fusion.49
  270.2 3.1 fusion.49
  283.8 3.1 fusion.49
  311.0 3.1 fusion.49
  324.6 3.1 fusion.49
  351.9 3.1 fusion.49
  365.5 3.1 fusion.49
  368.6 16.3 %pmax.7 = bf16[4,4,128,7]{2,0,3,1:T(4,128)(2,1)S(1)} all-reduce(bf16[4,4,128,7]{2,0,3,1:T(4,128)(2,1)S(1)} %copy.86), channel_id=1, replica_groups=mesh['replica'=8,'ctx'=4] {'ctx'}, use_global_device_ids=true, to_apply=%region_9.10 | all-reduce | flops 14336 | bytes 57344 | tf_op jit(solution)/shard_map/pmax | solution.py:134
  389.0 6.2 %multiply_convert_fusion.6 = bf16[4,4,128,7,128]{2,4,3,1,0:T(8,128)(2,1)} fusion(f32[4,4,128,7,128]{2,4,3,1,0:T(8,128)} %bitcast.16, f32[4,4,128,7]{2,3,1,0:T(8,128)S(1)} %copy.59), kind=kLoop, calls=%fused_computation.39 | loop fusion | flops 3670016 | bytes 11067392 | tf_op jit(solution)/shard_map/convert_element_type | solution.py:144
  395.2 7.3 %copy.60 = bf16[4,128,3584]{2,0,1:T(4,128)(2,1)} copy(bf16[4,128,3584]{1,2,0:T(8,128)(2,1)} %bitcast.135) | data formatting | bytes 7340032 | tf_op jit(solution)/shard_map/convert_element_type | solution.py:144
  404.5 6.8 %reduce-scatter.4.cloned.1.call-done = bf16[32,112]{1,0:T(8,128)(2,1)} async-done(((bf16[128,112]{1,0:T(8,128)(2,1)}), bf16[32,112]{1,0:T(8,128)(2,1)}) %reduce-scatter.4.cloned.1.call-update) | async-done | bytes 7184
  415.2 94.9 %all-reduce.3.cloned.1.call-done = bf16[4,128,3584]{2,0,1:T(4,128)(2,1)} async-done(((bf16[4,128,3584]{2,0,1:T(4,128)(2,1)}), bf16[4,128,3584]{2,0,1:T(4,128)(2,1)}) %all-reduce.3.cloned.1.call-update) | async-done | bytes 3670032
  (320 shorter events, 167.8 us)
Async XLA Ops:
  6.5 1.2 copy-start
  8.7 8.2 %copy-start.3 = (s32[32]{0:T(128)S(1)}, s32[32]{0:T(128)}, u32[]{:S(2)}) copy-start(s32[32]{0:T(128)} %param.15) | copy-start | bytes 388
  10.5 49.8 %all-to-all-start = ((bf16[8,32,3584]{2,1,0:T(8,128)(2,1)}), bf16[8,32,3584]{2,1,0:T(8,128)(2,1)S(1)}, u32[]{:S(2)}, u32[]{:S(2)}) async-start(bf16[8,32,3584]{2,1,0:T(8,128)(2,1)} %copy.51), calls=%async_computation | async-start | bytes 3670016 | tf_op jit(solution)/shard_map/all_to_all | solution.py:52
  16.9 394.4 %reduce-scatter.4.cloned.1.call-start = ((), (), s32[]{:S(2)}) async-start(), calls=%async_computation.2 | async-start | bytes 40960
  62.3 21.9 %collective-permute-start = (bf16[1,4,32,3584]{3,1,2,0:T(4,128)(2,1)S(1)}, bf16[1,4,32,3584]{3,1,2,0:T(4,128)(2,1)S(1)}, u32[]{:S(2)}, u32[]{:S(2)}) collective-permute-start(bf16[1,4,32,3584]{3,1,2,0:T(4,128)(2,1)S(1)} %bitcast.137), channel_id=1, source_target_pairs={{0,1},{1,0},{2,3},{3,2},{4,5},{5,4},{6,7},{7,6},{8,9},{9,8},{10,11... | collective-permute-start | bytes 2752520 | tf_op jit(solution)/shard_map/ppermute | solution.py:19
  87.8 40.9 %collective-permute-start.1 = (bf16[2,4,32,3584]{3,1,2,0:T(4,128)(2,1)}, bf16[2,4,32,3584]{3,1,2,0:T(4,128)(2,1)}, u32[]{:S(2)}, u32[]{:S(2)}) collective-permute-start(bf16[2,4,32,3584]{3,1,2,0:T(4,128)(2,1)} %get-tuple-element.372), channel_id=1, source_target_pairs={{0,2},{1,3},{2,0},{3,1},{4,6},{5,7},{6,4},{7,5},{8,10},{9,11},{10,... | collective-permute-start | bytes 5505032 | tf_op jit(solution)/shard_map/ppermute | solution.py:19
  91.4 7.2 %copy-start.2 = (s32[28,32,32]{2,1,0:T(8,128)S(1)}, s32[28,32,32]{2,1,0:T(8,128)}, u32[]{:S(2)}) copy-start(s32[28,32,32]{2,1,0:T(8,128)} %param.14) | copy-start | bytes 344068
  388.9 121.2 %all-reduce.3.cloned.1.call-start = ((), (), s32[]{:S(2)}) async-start(), calls=%async_computation.3 | async-start | bytes 7340032
  402.5 0.7 copy-start.4
  413.6 100.7 %copy-start.1 = (bf16[4,32,3584]{2,1,0:T(8,128)(2,1)S(1)}, bf16[4,32,3584]{2,1,0:T(8,128)(2,1)}, u32[]{:S(2)}) copy-start(bf16[4,32,3584]{2,1,0:T(8,128)(2,1)} %param.9) | copy-start | bytes 2752516
Sparse Core Ops, SparseCore 0:
  389.0 22.1 reduce-scatter.3
  414.4 95.6 all-reduce.2
